TPU v7x, 32 devices: a whole 2x2x4 slice. The times are simulated.
32 devices in a mesh: outer: 2 (over x), dp: 16 (over z, y, core).
Axes of the slice: x: 2, y: 2, z: 4, core: 2. Of those that a mesh axis runs over, the one named last changes fastest.
Arguments:
- fast_weights: float32 [2, 4096, 2048], P('outer', 'dp'), may hold values from -6 to 6
- slow_weights: float32 [4096, 2048], P('dp', 'outer'), may hold values from -6 to 6
- momentum: float32 [4096, 2048], P('dp', 'outer'), may hold values from -3 to 3
- tokens: bfloat16 [24576, 4096], P(('outer', 'dp')), may hold values from -6 to 6
- norm_gain: float32 [4096], replicated, may hold values from 0.1 to 1.9
Outputs:
- slow_next: float32 [4096, 2048], P('dp', 'outer')
- momentum_next: float32 [4096, 2048], P('dp', 'outer')
- fast_next: float32 [4096, 2048], P('dp')
- key_values: bfloat16 [24576, 2048], P(('outer', 'dp'))
All inputs are finite; a program needn't handle non-finite values.
Results may differ from a plain program's by a relative error of at most 0.0057.
Values may be sent and summed in bfloat16 or wider, within the bound.
No kernel may reach another device: no remote copies, remote signals or barrier semaphores. Data moves between devices by JAX's collectives and lax.ppermute only.
A program may use at most 128 MiB of HBM per device.

v0:
```python
import jax
import jax.numpy as jnp
from jax import lax
from jax.sharding import PartitionSpec as P

OUTER_LR = 0.7
MOMENTUM_COEF = 0.9
EPSILON = 1e-05


def outer_update(slow_part, moment_part, fast_total, pod_count):
    outer_grad = slow_part - fast_total / pod_count
    moment_next = MOMENTUM_COEF * moment_part + outer_grad
    slow_next = slow_part - OUTER_LR * (outer_grad + MOMENTUM_COEF * moment_next)
    return (slow_next, moment_next)


def body(fast_weights, slow_weights, momentum, tokens, norm_gain):
    pod_count = lax.axis_size("outer")
    width = tokens.shape[1]
    fast_total = lax.psum_scatter(fast_weights[0], "outer", scatter_dimension=1, tiled=True)
    slow_next, momentum_next = outer_update(slow_weights, momentum, fast_total, pod_count)
    fast_next = lax.all_gather(slow_next, "outer", axis=1, tiled=True)
    values = tokens.astype(jnp.float32)
    meansq = jnp.mean(values * values, axis=-1, keepdims=True)
    normed = (values * lax.rsqrt(meansq + EPSILON) * norm_gain).astype(jnp.bfloat16)
    whole_weights = lax.all_gather(fast_next.astype(jnp.bfloat16), "dp", axis=0, tiled=True)
    product = jnp.dot(normed, whole_weights, preferred_element_type=jnp.float32)
    key_values = (product * width ** (-0.5)).astype(jnp.bfloat16)
    return (slow_next, momentum_next, fast_next, key_values)


def solution(mesh):
    in_specs = (
        P("outer", "dp", None),
        P("dp", "outer"),
        P("dp", "outer"),
        P(("outer", "dp"), None),
        P(),
    )
    out_specs = (P("dp", "outer"), P("dp", "outer"), P("dp", None), P(("outer", "dp"), None))
    return jax.shard_map(body, mesh=mesh, in_specs=in_specs, out_specs=out_specs, check_vma=False)
```

profile of v0, /device:TPU:0, one launch (start us, length us, event | category | flops | bytes accessed | tf_op | source)
XLA Modules:
  0.0 238.8 jit_solution(7820645311359404585)
XLA Ops:
  7.2 0.0 reduce-scatter.2.cloned.1.call-start
  7.2 0.7 reduce-scatter.2.cloned.1.call-update
  7.9 0.0 all-gather.3.cloned.1.call-start
  7.9 36.9 %reduce-scatter.2.cloned.1.call-done = f32[256,1024]{1,0:T(8,128)} async-done(((f32[256,2048]{1,0:T(8,128)}), f32[256,1024]{1,0:T(8,128)}) %reduce-scatter.2.cloned.1.call-update) | async-done | bytes 1048592 | tf_op jit(solution)/shard_map/reduce_scatter | solution.py:21
  44.9 3.7 %multiply_subtract_fusion = (f32[256,1024]{1,0:T(8,128)}, f32[256,1024]{1,0:T(8,128)}) fusion(f32[256,1024]{1,0:T(8,128)} %param.6, f32[256,1024]{1,0:T(8,128)} %reduce-scatter.2.cloned.1.call-done, f32[256,1024]{1,0:T(8,128)} %param.7), kind=kLoop, calls=%fused_computation.9 | loop fusion | flops 2097152 | bytes 5242880 | tf_op jit(solution)/shard_map/sub | solution.py:14
  48.6 0.0 copy-start.1
  48.6 0.0 all-gather.3.cloned.1.call-update
  48.6 0.0 all-gather.5.cloned.1.call-start
  48.7 33.2 %all-gather.3.cloned.1.call-done = f32[256,2048]{1,0:T(8,128)} async-done(((f32[256,1024]{1,0:T(8,128)}), f32[256,2048]{1,0:T(8,128)}) %all-gather.3.cloned.1.call-update) | async-done | bytes 2097168 | tf_op jit(solution)/shard_map/all_gather | solution.py:23
  81.9 2.7 %convert_element_type.14 = bf16[256,2048]{1,0:T(8,128)(2,1)} convert(f32[256,2048]{1,0:T(8,128)} %all-gather.3.cloned.1.call-done) | non-fusion elementwise | flops 524288 | bytes 3145728 | tf_op jit(solution)/shard_map/convert_element_type | solution.py:27
  84.6 0.0 all-gather.5.cloned.1.call-update
  84.6 4.1 %fusion = f32[768]{0:T(1024)S(1)} fusion(bf16[768,4096]{1,0:T(8,128)(2,1)} %param.8), kind=kLoop, calls=%fused_computation.2 | loop fusion | flops 9436416 | bytes 6294528 | tf_op jit(solution)/shard_map/reduce_sum | solution.py:25
  88.7 0.0 copy-start
  88.7 122.5 %all-gather.5.cloned.1.call-done = bf16[4096,2048]{1,0:T(8,128)(2,1)} async-done(((bf16[256,2048]{1,0:T(8,128)(2,1)}), bf16[4096,2048]{1,0:T(8,128)(2,1)}) %all-gather.5.cloned.1.call-update) | async-done | bytes 16777232 | tf_op jit(solution)/shard_map/all_gather | solution.py:27
  211.2 0.0 copy-done.1
  211.2 19.7 %multiply_convert_fusion = bf16[768,2048]{1,0:T(8,128)(2,1)} fusion(bf16[4096,2048]{1,0:T(8,128)(2,1)} %all-gather.5.cloned.1.call-done, bf16[768,4096]{1,0:T(8,128)(2,1)} %param.8, f32[4096]{0:T(1024)S(1)} %copy-done.1, f32[768]{0:T(1024)S(1)} %add_rsqrt_fusion), kind=kOutput, calls=%fused_computation.6 | convolution fusion | flops 12900630528 | bytes 26233856 | tf_op jit(solution)/shard_map/dot_general | solution.py:28
  231.0 0.0 copy-done
  231.0 1.3 copy.10
  (1 shorter events, 0.0 us)
Async XLA Ops:
  7.2 37.7 %reduce-scatter.2.cloned.1.call-start = ((), (), s32[]{:S(2)}) async-start(), calls=%async_computation.1 | async-start | bytes 3145728 | tf_op jit(solution)/shard_map/reduce_scatter | solution.py:21
  7.9 74.0 %all-gather.3.cloned.1.call-start = ((), (), s32[]{:S(2)}) async-start(), calls=%async_computation.2 | async-start | bytes 3145728 | tf_op jit(solution)/shard_map/all_gather | solution.py:23
  48.6 162.6 %copy-start.1 = (f32[4096]{0:T(1024)S(1)}, f32[4096]{0:T(1024)}, u32[]{:S(2)}) copy-start(f32[4096]{0:T(1024)} %param.9) | copy-start | bytes 49156
  48.6 162.6 %all-gather.5.cloned.1.call-start = ((), (), s32[]{:S(2)}) async-start(), calls=%async_computation.3 | async-start | bytes 17825792 | tf_op jit(solution)/shard_map/all_gather | solution.py:27
  88.7 142.3 %copy-start = (f32[256,2048]{1,0:T(8,128)S(1)}, f32[256,2048]{1,0:T(8,128)}, u32[]{:S(2)}) copy-start(f32[256,2048]{1,0:T(8,128)} %all-gather.3.cloned.1.call-done) | copy-start | bytes 6291460
Sparse Core Ops, SparseCore 0:
  10.2 34.6 reduce-scatter.1
  48.7 33.0 all-gather.2
  84.7 126.4 all-gather.4
where the time goes:
time: 239 us
  waiting for transfers between devices  193 us (81%)
  matrix products  19.7 us (8%)
  between operations  13.8 us (6%)
  other arithmetic  10.5 us (4%)
    all_gather x1, waiting for transfers between devices, body(): lax.all_gather(fast_next.astype(jnp.bfloat16), 'dp', axis=0, tiled=True)  122 us
    reduce_scatter x1, waiting for transfers between devices, body(): lax.psum_scatter(fast_weights[0], 'outer', scatter_dimension=1, tiled=True)  36.9 us
    all_gather x1, waiting for transfers between devices, body(): fast_next = lax.all_gather(slow_next, 'outer', axis=1, tiled=True)  33.2 us
    dot_general x1, matrix products, body(): product = jnp.dot(normed, whole_weights, preferred_element_type=jnp.float32)  19.7 us
  transfers between devices with their start and end apart: 3, of which 3 were waited for; matrix products, arithmetic and copies ran while one was open for 2% of the time, Pallas kernels for 0%

commit v1 on v0

--- a/solution.py
+++ b/solution.py
@@ -24,7 +24,24 @@
     values = tokens.astype(jnp.float32)
     meansq = jnp.mean(values * values, axis=-1, keepdims=True)
     normed = (values * lax.rsqrt(meansq + EPSILON) * norm_gain).astype(jnp.bfloat16)
-    whole_weights = lax.all_gather(fast_next.astype(jnp.bfloat16), "dp", axis=0, tiled=True)
+    x = fast_next.astype(jnp.bfloat16)
+    length, index, span = (lax.axis_size("dp"), lax.axis_index("dp"), x.shape[0])
+    right = [(i, (i + 1) % length) for i in range(length)]
+    behind = [(i, (i - 1) % length) for i in range(length)]
+    whole_weights = jnp.zeros((*x.shape[:0], length * span, *x.shape[0 + 1 :]), x.dtype)
+    whole_weights = lax.dynamic_update_slice_in_dim(whole_weights, x, index * span, axis=0)
+    from_left = from_right = x
+    half = length // 2
+    for step in range(1, half + 1):
+        from_left = lax.ppermute(from_left, "dp", right)
+        whole_weights = lax.dynamic_update_slice_in_dim(
+            whole_weights, from_left, (index - step) % length * span, axis=0
+        )
+        if step < length - half:
+            from_right = lax.ppermute(from_right, "dp", behind)
+            whole_weights = lax.dynamic_update_slice_in_dim(
+                whole_weights, from_right, (index + step) % length * span, axis=0
+            )
     product = jnp.dot(normed, whole_weights, preferred_element_type=jnp.float32)
     key_values = (product * width ** (-0.5)).astype(jnp.bfloat16)
     return (slow_next, momentum_next, fast_next, key_values)

time: 239 us -> 309 us (1.29)
  the two profiles are of different devices: /device:TPU:0 before, /device:TPU:1 now
where the time goes in v1:
time: 309 us; the launch traced here: 308 us
  waiting for transfers between devices  211 us (68%)
  local copies, waits for them, and re-layouts  38.2 us (12%)
  matrix products  19.7 us (6%)
  starting transfers between devices  19.4 us (6%)
  between operations  14.1 us (5%)
  other arithmetic  6.27 us (2%)
    ppermute x8, waiting for transfers between devices, body(): from_left = lax.ppermute(from_left, 'dp', right)  85.4 us
    ppermute x7, waiting for transfers between devices, body(): from_right = lax.ppermute(from_right, 'dp', behind)  55.1 us
    reduce_scatter x1, waiting for transfers between devices, body(): lax.psum_scatter(fast_weights[0], 'outer', scatter_dimension=1, tiled=True)  36.1 us
    all_gather x1, waiting for transfers between devices, body(): fast_next = lax.all_gather(slow_next, 'outer', axis=1, tiled=True)  33.2 us
    dot_general x1, matrix products, body(): product = jnp.dot(normed, whole_weights, preferred_element_type=jnp.float32)  19.7 us
    ppermute x8, starting transfers between devices, body(): from_left = lax.ppermute(from_left, 'dp', right)  19.3 us
    dynamic_update_slice x8, local copies, waits for them, and re-layouts, body(): lax.dynamic_update_slice_in_dim(whole_weights, from_left, (index - step)...  14.9 us
    dynamic_update_slice x7, local copies, waits for them, and re-layouts, body(): lax.dynamic_update_slice_in_dim(whole_weights, from_right, (index + step)...  13.9 us
  transfers between devices with their start and end apart: 17, of which 16 were waited for; matrix products, arithmetic and copies ran while one was open for 9% of the time, Pallas kernels for 0%

profile of v1, /device:TPU:1, one launch (start us, length us, event | category | flops | bytes accessed | tf_op | source)
XLA Modules:
  0.0 308.3 jit_solution(7799758165588863300)
XLA Ops:
  7.9 36.1 %reduce-scatter.2.cloned.1.call-done = f32[256,1024]{1,0:T(8,128)} async-done(((f32[256,2048]{1,0:T(8,128)}), f32[256,1024]{1,0:T(8,128)}) %reduce-scatter.2.cloned.1.call-update) | async-done | bytes 1048592 | tf_op jit(solution)/shard_map/reduce_scatter | solution.py:21
  44.1 3.7 %multiply_subtract_fusion = (f32[256,1024]{1,0:T(8,128)}, f32[256,1024]{1,0:T(8,128)}) fusion(f32[256,1024]{1,0:T(8,128)} %param.6, f32[256,1024]{1,0:T(8,128)} %reduce-scatter.2.cloned.1.call-done, f32[256,1024]{1,0:T(8,128)} %param.7), kind=kLoop, calls=%fused_computation.9 | loop fusion | flops 2097152 | bytes 5242880 | tf_op jit(solution)/shard_map/sub | solution.py:14
  47.8 33.2 %all-gather.2.cloned.1.call-done = f32[256,2048]{1,0:T(8,128)} async-done(((f32[256,1024]{1,0:T(8,128)}), f32[256,2048]{1,0:T(8,128)}) %all-gather.2.cloned.1.call-update) | async-done | bytes 2097168 | tf_op jit(solution)/shard_map/all_gather | solution.py:23
  81.1 8.1 %broadcast_in_dim.2 = bf16[4096,2048]{1,0:T(8,128)(2,1)} broadcast(bf16[]{:T(256)} %constant.104.clone.1), dimensions={} | broadcast | bytes 16777218 | tf_op jit(solution)/shard_map/broadcast_in_dim | solution.py:31
  92.3 23.0 %collective-permute-done = bf16[256,2048]{1,0:T(8,128)(2,1)S(1)} collective-permute-done((bf16[256,2048]{1,0:T(8,128)(2,1)S(1)}, bf16[256,2048]{1,0:T(8,128)(2,1)S(1)}, u32[]{:S(2)}, u32[]{:S(2)}) %collective-permute-start) | collective-permute-done | bytes 1048608 | tf_op jit(solution)/shard_map/ppermute | solution.py:36
  115.3 2.5 collective-permute-start.2
  117.8 11.2 %collective-permute-done.1 = bf16[256,2048]{1,0:T(8,128)(2,1)S(1)} collective-permute-done((bf16[256,2048]{1,0:T(8,128)(2,1)S(1)}, bf16[256,2048]{1,0:T(8,128)(2,1)S(1)}, u32[]{:S(2)}, u32[]{:S(2)}) %collective-permute-start.1) | collective-permute-done | bytes 1048608 | tf_op jit(solution)/shard_map/ppermute | solution.py:41
  129.0 10.9 %collective-permute-done.2 = bf16[256,2048]{1,0:T(8,128)(2,1)S(1)} collective-permute-done((bf16[256,2048]{1,0:T(8,128)(2,1)S(1)}, bf16[256,2048]{1,0:T(8,128)(2,1)S(1)}, u32[]{:S(2)}, u32[]{:S(2)}) %collective-permute-start.2) | collective-permute-done | bytes 1048608 | tf_op jit(solution)/shard_map/ppermute | solution.py:36
  139.9 2.5 collective-permute-start.4
  142.4 12.0 %collective-permute-done.3 = bf16[256,2048]{1,0:T(8,128)(2,1)S(1)} collective-permute-done((bf16[256,2048]{1,0:T(8,128)(2,1)S(1)}, bf16[256,2048]{1,0:T(8,128)(2,1)S(1)}, u32[]{:S(2)}, u32[]{:S(2)}) %collective-permute-start.3) | collective-permute-done | bytes 1048608 | tf_op jit(solution)/shard_map/ppermute | solution.py:41
  154.3 10.2 %collective-permute-done.4 = bf16[256,2048]{1,0:T(8,128)(2,1)S(1)} collective-permute-done((bf16[256,2048]{1,0:T(8,128)(2,1)S(1)}, bf16[256,2048]{1,0:T(8,128)(2,1)S(1)}, u32[]{:S(2)}, u32[]{:S(2)}) %collective-permute-start.4) | collective-permute-done | bytes 1048608 | tf_op jit(solution)/shard_map/ppermute | solution.py:36
  164.6 2.5 collective-permute-start.6
  167.0 10.7 %collective-permute-done.5 = bf16[256,2048]{1,0:T(8,128)(2,1)S(1)} collective-permute-done((bf16[256,2048]{1,0:T(8,128)(2,1)S(1)}, bf16[256,2048]{1,0:T(8,128)(2,1)S(1)}, u32[]{:S(2)}, u32[]{:S(2)}) %collective-permute-start.5) | collective-permute-done | bytes 1048608 | tf_op jit(solution)/shard_map/ppermute | solution.py:41
  177.7 11.4 %collective-permute-done.6 = bf16[256,2048]{1,0:T(8,128)(2,1)S(1)} collective-permute-done((bf16[256,2048]{1,0:T(8,128)(2,1)S(1)}, bf16[256,2048]{1,0:T(8,128)(2,1)S(1)}, u32[]{:S(2)}, u32[]{:S(2)}) %collective-permute-start.6) | collective-permute-done | bytes 1048608 | tf_op jit(solution)/shard_map/ppermute | solution.py:36
  189.2 2.5 collective-permute-start.8
  191.7 9.5 %collective-permute-done.7 = bf16[256,2048]{1,0:T(8,128)(2,1)} collective-permute-done((bf16[256,2048]{1,0:T(8,128)(2,1)S(1)}, bf16[256,2048]{1,0:T(8,128)(2,1)}, u32[]{:S(2)}, u32[]{:S(2)}) %collective-permute-start.7) | collective-permute-done | bytes 1048608 | tf_op jit(solution)/shard_map/ppermute | solution.py:41
  202.5 10.5 %collective-permute-done.8 = bf16[256,2048]{1,0:T(8,128)(2,1)} collective-permute-done((bf16[256,2048]{1,0:T(8,128)(2,1)S(1)}, bf16[256,2048]{1,0:T(8,128)(2,1)}, u32[]{:S(2)}, u32[]{:S(2)}) %collective-permute-start.8) | collective-permute-done | bytes 1048608 | tf_op jit(solution)/shard_map/ppermute | solution.py:36
  213.0 2.6 collective-permute-start.10
  215.6 2.4 constant_dynamic-update-slice_fusion.14
  218.0 2.3 constant_dynamic-update-slice_fusion.13
  222.6 4.4 %collective-permute-done.9 = bf16[256,2048]{1,0:T(8,128)(2,1)} collective-permute-done((bf16[256,2048]{1,0:T(8,128)(2,1)}, bf16[256,2048]{1,0:T(8,128)(2,1)}, u32[]{:S(2)}, u32[]{:S(2)}) %collective-permute-start.9) | collective-permute-done | bytes 1048608 | tf_op jit(solution)/shard_map/ppermute | solution.py:41
  229.3 9.7 %collective-permute-done.10 = bf16[256,2048]{1,0:T(8,128)(2,1)} collective-permute-done((bf16[256,2048]{1,0:T(8,128)(2,1)}, bf16[256,2048]{1,0:T(8,128)(2,1)}, u32[]{:S(2)}, u32[]{:S(2)}) %collective-permute-start.10) | collective-permute-done | bytes 1048608 | tf_op jit(solution)/shard_map/ppermute | solution.py:36
  238.9 2.5 collective-permute-start.12
  242.5 2.3 constant_dynamic-update-slice_fusion.9
  247.2 2.3 constant_dynamic-update-slice_fusion.7
  249.5 3.1 %collective-permute-done.11 = bf16[256,2048]{1,0:T(8,128)(2,1)S(1)} collective-permute-done((bf16[256,2048]{1,0:T(8,128)(2,1)}, bf16[256,2048]{1,0:T(8,128)(2,1)S(1)}, u32[]{:S(2)}, u32[]{:S(2)}) %collective-permute-start.11) | collective-permute-done | bytes 1048608 | tf_op jit(solution)/shard_map/ppermute | solution.py:41
  252.6 2.4 constant_dynamic-update-slice_fusion.6
  255.0 9.7 %collective-permute-done.12 = bf16[256,2048]{1,0:T(8,128)(2,1)S(1)} collective-permute-done((bf16[256,2048]{1,0:T(8,128)(2,1)}, bf16[256,2048]{1,0:T(8,128)(2,1)S(1)}, u32[]{:S(2)}, u32[]{:S(2)}) %collective-permute-start.12) | collective-permute-done | bytes 1048608 | tf_op jit(solution)/shard_map/ppermute | solution.py:36
  264.7 2.4 collective-permute-start.14
  269.4 2.3 constant_dynamic-update-slice_fusion.4
  273.9 4.2 %collective-permute-done.13 = bf16[256,2048]{1,0:T(8,128)(2,1)S(1)} collective-permute-done((bf16[256,2048]{1,0:T(8,128)(2,1)S(1)}, bf16[256,2048]{1,0:T(8,128)(2,1)S(1)}, u32[]{:S(2)}, u32[]{:S(2)}) %collective-permute-start.13) | collective-permute-done | bytes 1048608 | tf_op jit(solution)/shard_map/ppermute | solution.py:41
  280.4 19.7 %multiply_convert_fusion = bf16[768,2048]{1,0:T(8,128)(2,1)} fusion(bf16[4096,2048]{1,0:T(8,128)(2,1)} %constant_dynamic-update-slice_fusion, bf16[768,4096]{1,0:T(8,128)(2,1)} %param.8, f32[4096]{0:T(1024)S(1)} %copy-done.8, f32[768]{0:T(1024)S(1)} %add_rsqrt_fusion), kind=kOutput, calls=%fused_computation.6 | convolution fusion | flops 12900630528 | bytes 26233856 | tf_op jit(solution)/shard_map/dot_general | solution.py:45
  (44 shorter events, 21.4 us)
Async XLA Ops:
  7.2 36.9 %reduce-scatter.2.cloned.1.call-start = ((), (), s32[]{:S(2)}) async-start(), calls=%async_computation.1 | async-start | bytes 3145728 | tf_op jit(solution)/shard_map/reduce_scatter | solution.py:21
  7.9 73.2 %all-gather.2.cloned.1.call-start = ((), (), s32[]{:S(2)}) async-start(), calls=%async_computation.2 | async-start | bytes 3145728 | tf_op jit(solution)/shard_map/all_gather | solution.py:23
  81.1 8.1 %copy-start = (f32[256,2048]{1,0:T(8,128)S(1)}, f32[256,2048]{1,0:T(8,128)}, u32[]{:S(2)}) copy-start(f32[256,2048]{1,0:T(8,128)} %all-gather.2.cloned.1.call-done) | copy-start | bytes 6291460
  81.1 120.1 %copy-start.1 = (bf16[768,4096]{1,0:T(8,128)(2,1)S(1)}, bf16[768,4096]{1,0:T(8,128)(2,1)}, u32[]{:S(2)}) copy-start(bf16[768,4096]{1,0:T(8,128)(2,1)} %param.8) | copy-start | bytes 18874372
  90.4 24.9 %collective-permute-start = (bf16[256,2048]{1,0:T(8,128)(2,1)S(1)}, bf16[256,2048]{1,0:T(8,128)(2,1)S(1)}, u32[]{:S(2)}, u32[]{:S(2)}) collective-permute-start(bf16[256,2048]{1,0:T(8,128)(2,1)S(1)} %get-tuple-element.5), channel_id=1, source_target_pairs={{0,1},{1,2},{2,3},{3,4},{4,5},{5,6},{6,7},{7,8},{8,9},{9,10},{10,1... | collective-permute-start | bytes 3145736 | tf_op jit(solution)/shard_map/ppermute | solution.py:36
  92.3 36.7 %collective-permute-start.1 = (bf16[256,2048]{1,0:T(8,128)(2,1)S(1)}, bf16[256,2048]{1,0:T(8,128)(2,1)S(1)}, u32[]{:S(2)}, u32[]{:S(2)}) collective-permute-start(bf16[256,2048]{1,0:T(8,128)(2,1)S(1)} %get-tuple-element.5), channel_id=1, source_target_pairs={{0,15},{1,0},{2,1},{3,2},{4,3},{5,4},{6,5},{7,6},{8,7},{9,8},{10,9... | collective-permute-start | bytes 3145736 | tf_op jit(solution)/shard_map/ppermute | solution.py:41
  115.3 73.9 %copy-start.2 = (bf16[256,2048]{1,0:T(8,128)(2,1)}, bf16[256,2048]{1,0:T(8,128)(2,1)S(1)}, u32[]{:S(2)}) copy-start(bf16[256,2048]{1,0:T(8,128)(2,1)S(1)} %collective-permute-done) | copy-start | bytes 3145732
  115.3 24.6 %collective-permute-start.2 = (bf16[256,2048]{1,0:T(8,128)(2,1)S(1)}, bf16[256,2048]{1,0:T(8,128)(2,1)S(1)}, u32[]{:S(2)}, u32[]{:S(2)}) collective-permute-start(bf16[256,2048]{1,0:T(8,128)(2,1)S(1)} %collective-permute-done), channel_id=1, source_target_pairs={{0,1},{1,2},{2,3},{3,4},{4,5},{5,6},{6,7},{7,8},{8,9},{9,10},{10,1... | collective-permute-start | bytes 3145736 | tf_op jit(solution)/shard_map/ppermute | solution.py:36
  129.0 13.3 %copy-start.4 = (bf16[256,2048]{1,0:T(8,128)(2,1)}, bf16[256,2048]{1,0:T(8,128)(2,1)S(1)}, u32[]{:S(2)}) copy-start(bf16[256,2048]{1,0:T(8,128)(2,1)S(1)} %collective-permute-done.1) | copy-start | bytes 3145732
  129.0 25.3 %collective-permute-start.3 = (bf16[256,2048]{1,0:T(8,128)(2,1)S(1)}, bf16[256,2048]{1,0:T(8,128)(2,1)S(1)}, u32[]{:S(2)}, u32[]{:S(2)}) collective-permute-start(bf16[256,2048]{1,0:T(8,128)(2,1)S(1)} %collective-permute-done.1), channel_id=1, source_target_pairs={{0,15},{1,0},{2,1},{3,2},{4,3},{5,4},{6,5},{7,6},{8,7},{9,8},{10,9... | collective-permute-start | bytes 3145736 | tf_op jit(solution)/shard_map/ppermute | solution.py:41
  139.9 61.3 %copy-start.7 = (bf16[256,2048]{1,0:T(8,128)(2,1)}, bf16[256,2048]{1,0:T(8,128)(2,1)S(1)}, u32[]{:S(2)}) copy-start(bf16[256,2048]{1,0:T(8,128)(2,1)S(1)} %collective-permute-done.2) | copy-start | bytes 3145732
  139.9 24.7 %collective-permute-start.4 = (bf16[256,2048]{1,0:T(8,128)(2,1)S(1)}, bf16[256,2048]{1,0:T(8,128)(2,1)S(1)}, u32[]{:S(2)}, u32[]{:S(2)}) collective-permute-start(bf16[256,2048]{1,0:T(8,128)(2,1)S(1)} %collective-permute-done.2), channel_id=1, source_target_pairs={{0,1},{1,2},{2,3},{3,4},{4,5},{5,6},{6,7},{7,8},{8,9},{9,10},{10,1... | collective-permute-start | bytes 3145736 | tf_op jit(solution)/shard_map/ppermute | solution.py:36
  154.3 46.9 %copy-start.5 = (bf16[256,2048]{1,0:T(8,128)(2,1)}, bf16[256,2048]{1,0:T(8,128)(2,1)S(1)}, u32[]{:S(2)}) copy-start(bf16[256,2048]{1,0:T(8,128)(2,1)S(1)} %collective-permute-done.3) | copy-start | bytes 3145732
  154.3 23.4 %collective-permute-start.5 = (bf16[256,2048]{1,0:T(8,128)(2,1)S(1)}, bf16[256,2048]{1,0:T(8,128)(2,1)S(1)}, u32[]{:S(2)}, u32[]{:S(2)}) collective-permute-start(bf16[256,2048]{1,0:T(8,128)(2,1)S(1)} %collective-permute-done.3), channel_id=1, source_target_pairs={{0,15},{1,0},{2,1},{3,2},{4,3},{5,4},{6,5},{7,6},{8,7},{9,8},{10,9... | collective-permute-start | bytes 3145736 | tf_op jit(solution)/shard_map/ppermute | solution.py:41
  164.6 24.6 %collective-permute-start.6 = (bf16[256,2048]{1,0:T(8,128)(2,1)S(1)}, bf16[256,2048]{1,0:T(8,128)(2,1)S(1)}, u32[]{:S(2)}, u32[]{:S(2)}) collective-permute-start(bf16[256,2048]{1,0:T(8,128)(2,1)S(1)} %collective-permute-done.4), channel_id=1, source_target_pairs={{0,1},{1,2},{2,3},{3,4},{4,5},{5,6},{6,7},{7,8},{8,9},{9,10},{10,1... | collective-permute-start | bytes 3145736 | tf_op jit(solution)/shard_map/ppermute | solution.py:36
  177.7 13.9 %copy-start.3 = (bf16[256,2048]{1,0:T(8,128)(2,1)}, bf16[256,2048]{1,0:T(8,128)(2,1)S(1)}, u32[]{:S(2)}) copy-start(bf16[256,2048]{1,0:T(8,128)(2,1)S(1)} %collective-permute-done.5) | copy-start | bytes 3145732
  177.7 23.4 %collective-permute-start.7 = (bf16[256,2048]{1,0:T(8,128)(2,1)S(1)}, bf16[256,2048]{1,0:T(8,128)(2,1)}, u32[]{:S(2)}, u32[]{:S(2)}) collective-permute-start(bf16[256,2048]{1,0:T(8,128)(2,1)S(1)} %collective-permute-done.5), channel_id=1, source_target_pairs={{0,15},{1,0},{2,1},{3,2},{4,3},{5,4},{6,5},{7,6},{8,7},{9,8},{10,9... | collective-permute-start | bytes 3145736 | tf_op jit(solution)/shard_map/ppermute | solution.py:41
  189.2 13.3 %copy-start.6 = (bf16[256,2048]{1,0:T(8,128)(2,1)}, bf16[256,2048]{1,0:T(8,128)(2,1)S(1)}, u32[]{:S(2)}) copy-start(bf16[256,2048]{1,0:T(8,128)(2,1)S(1)} %collective-permute-done.6) | copy-start | bytes 3145732
  189.2 23.9 %collective-permute-start.8 = (bf16[256,2048]{1,0:T(8,128)(2,1)S(1)}, bf16[256,2048]{1,0:T(8,128)(2,1)}, u32[]{:S(2)}, u32[]{:S(2)}) collective-permute-start(bf16[256,2048]{1,0:T(8,128)(2,1)S(1)} %collective-permute-done.6), channel_id=1, source_target_pairs={{0,1},{1,2},{2,3},{3,4},{4,5},{5,6},{6,7},{7,8},{8,9},{9,10},{10,1... | collective-permute-start | bytes 3145736 | tf_op jit(solution)/shard_map/ppermute | solution.py:36
  201.2 25.8 %collective-permute-start.9 = (bf16[256,2048]{1,0:T(8,128)(2,1)}, bf16[256,2048]{1,0:T(8,128)(2,1)}, u32[]{:S(2)}, u32[]{:S(2)}) collective-permute-start(bf16[256,2048]{1,0:T(8,128)(2,1)} %collective-permute-done.7), channel_id=1, source_target_pairs={{0,15},{1,0},{2,1},{3,2},{4,3},{5,4},{6,5},{7,6},{8,7},{9,8},{10,9... | collective-permute-start | bytes 3145736 | tf_op jit(solution)/shard_map/ppermute | solution.py:41
  202.5 77.8 %copy-start.8 = (f32[4096]{0:T(1024)S(1)}, f32[4096]{0:T(1024)}, u32[]{:S(2)}) copy-start(f32[4096]{0:T(1024)} %param.9) | copy-start | bytes 49156
  213.0 25.9 %collective-permute-start.10 = (bf16[256,2048]{1,0:T(8,128)(2,1)}, bf16[256,2048]{1,0:T(8,128)(2,1)}, u32[]{:S(2)}, u32[]{:S(2)}) collective-permute-start(bf16[256,2048]{1,0:T(8,128)(2,1)} %collective-permute-done.8), channel_id=1, source_target_pairs={{0,1},{1,2},{2,3},{3,4},{4,5},{5,6},{6,7},{7,8},{8,9},{9,10},{10,1... | collective-permute-start | bytes 3145736 | tf_op jit(solution)/shard_map/ppermute | solution.py:36
  227.0 25.7 %collective-permute-start.11 = (bf16[256,2048]{1,0:T(8,128)(2,1)}, bf16[256,2048]{1,0:T(8,128)(2,1)S(1)}, u32[]{:S(2)}, u32[]{:S(2)}) collective-permute-start(bf16[256,2048]{1,0:T(8,128)(2,1)} %collective-permute-done.9), channel_id=1, source_target_pairs={{0,15},{1,0},{2,1},{3,2},{4,3},{5,4},{6,5},{7,6},{8,7},{9,8},{10,9... | collective-permute-start | bytes 3145736 | tf_op jit(solution)/shard_map/ppermute | solution.py:41
  238.9 25.8 %collective-permute-start.12 = (bf16[256,2048]{1,0:T(8,128)(2,1)}, bf16[256,2048]{1,0:T(8,128)(2,1)S(1)}, u32[]{:S(2)}, u32[]{:S(2)}) collective-permute-start(bf16[256,2048]{1,0:T(8,128)(2,1)} %collective-permute-done.10), channel_id=1, source_target_pairs={{0,1},{1,2},{2,3},{3,4},{4,5},{5,6},{6,7},{7,8},{8,9},{9,10},{10,1... | collective-permute-start | bytes 3145736 | tf_op jit(solution)/shard_map/ppermute | solution.py:36
  252.6 25.5 %collective-permute-start.13 = (bf16[256,2048]{1,0:T(8,128)(2,1)S(1)}, bf16[256,2048]{1,0:T(8,128)(2,1)S(1)}, u32[]{:S(2)}, u32[]{:S(2)}) collective-permute-start(bf16[256,2048]{1,0:T(8,128)(2,1)S(1)} %collective-permute-done.11), channel_id=1, source_target_pairs={{0,15},{1,0},{2,1},{3,2},{4,3},{5,4},{6,5},{7,6},{8,7},{9,8},{10,9... | collective-permute-start | bytes 3145736 | tf_op jit(solution)/shard_map/ppermute | solution.py:41
  264.7 14.6 %collective-permute-start.14 = (bf16[256,2048]{1,0:T(8,128)(2,1)S(1)}, bf16[256,2048]{1,0:T(8,128)(2,1)S(1)}, u32[]{:S(2)}, u32[]{:S(2)}) collective-permute-start(bf16[256,2048]{1,0:T(8,128)(2,1)S(1)} %collective-permute-done.12), channel_id=1, source_target_pairs={{0,1},{1,2},{2,3},{3,4},{4,5},{5,6},{6,7},{7,8},{8,9},{9,10},{10,1... | collective-permute-start | bytes 3145736 | tf_op jit(solution)/shard_map/ppermute | solution.py:36
Sparse Core Ops, SparseCore 0:
  10.2 33.7 reduce-scatter.1
  47.9 33.0 all-gather.1
